TPU v7x, 32 devices: a whole 2x2x4 slice. The times are simulated.
32 devices in a mesh: row: 8 (over y, x, core), col: 4 (over z).
Axes of the slice: x: 2, y: 2, z: 4, core: 2. Of those that a mesh axis runs over, the one named last changes fastest.
Arguments:
- tokens: bfloat16 [256, 8192], P('row', 'col'), may hold values from -6 to 6
- gate_codes: int32 [1024, 28672], P('col', 'row'), may hold values from -2147483648 to 2147483646
- up_codes: int32 [1024, 28672], P('col', 'row'), may hold values from -2147483648 to 2147483646
- down_codes: int32 [3584, 8192], P('row', 'col'), may hold values from -2147483648 to 2147483646
- gate_scales: bfloat16 [64, 28672], P('row'), may hold values from 0.0009994507 to 0.0049743652
- up_scales: bfloat16 [64, 28672], P('row'), may hold values from 0.0009994507 to 0.0049743652
- down_scales: bfloat16 [8192, 224], P('row'), may hold values from 0.00059890747 to 0.0029907227
Outputs:
- mixed: bfloat16 [256, 8192], P('row', 'col')
Inputs may be any that keep to these rules, and one draw needn't show every extreme that they name: Every word of gate_codes, up_codes and down_codes is an arbitrary 32-bit pattern: all sixteen codes occur in every nibble position.
All inputs are finite; a program needn't handle non-finite values.
Results may differ from a plain program's by a relative error of at most 0.025.
Values may be sent and summed in bfloat16 or wider, within the bound.
A program may use at most 192 MiB of HBM per device.

v0:
```python
import functools

import jax
import jax.numpy as jnp
from jax import lax
from jax.experimental import pallas as pl
from jax.experimental.pallas import tpu as pltpu
from jax.sharding import PartitionSpec as P

GROUP = 128
PACK = 8
SUB = GROUP // PACK


def tile_of(width, most):
    tile = (min(width, most) // 128) * 128
    while width % tile:
        tile -= 128
    return tile


def permutation():
    source = lax.broadcasted_iota(jnp.int32, (GROUP, GROUP), 0)
    target = lax.broadcasted_iota(jnp.int32, (GROUP, GROUP), 1)
    wanted = lax.rem(target, SUB) * PACK + lax.div(target, SUB)
    return (source == wanted).astype(jnp.bfloat16)


def permute_features(source_ref, target_ref):
    perm = permutation()
    for group in range(source_ref.shape[1] // GROUP):
        at = pl.ds(group * GROUP, GROUP)
        target_ref[:, at] = jnp.dot(
            source_ref[:, at], perm, preferred_element_type=jnp.float32
        ).astype(jnp.bfloat16)


def dequantize(codes_ref, scales_ref, dense_ref):
    def one(group, carry):
        word = codes_ref[pl.ds(pl.multiple_of(group * SUB, SUB), SUB), :] ^ jnp.int32(-2004318072)
        scale = scales_ref[pl.ds(group, 1), :]
        for k in range(PACK):
            code = word if k == PACK - 1 else jnp.left_shift(word, 28 - 4 * k)
            value = jnp.right_shift(code, 28).astype(jnp.float32)
            row = pl.multiple_of(group * GROUP + k * SUB, SUB)
            dense_ref[pl.ds(row, SUB), :] = (value * scale).astype(jnp.bfloat16)
        return carry

    lax.fori_loop(0, codes_ref.shape[0] // SUB, one, 0)


def up_kernel(tokens, gate, up, gate_scale, up_scale, out, moved, dense):
    @pl.when(pl.program_id(0) == 0)
    def _():
        permute_features(tokens, moved)

    for index, (codes, scale) in enumerate(((gate, gate_scale), (up, up_scale))):
        dequantize(codes, scale, dense.at[index])
        total = jnp.dot(moved[...], dense[index], preferred_element_type=jnp.float32)
        out[index] = total.astype(jnp.bfloat16)


def down_kernel(hidden, codes, scale, out, moved, dense):
    @pl.when(pl.program_id(0) == 0)
    def _():
        permute_features(hidden, moved)

    dequantize(codes, scale, dense)
    out[...] = jnp.dot(moved[...], dense[...], preferred_element_type=jnp.float32).astype(
        jnp.bfloat16
    )


PARAMS = dict(dimension_semantics=("arbitrary",), vmem_limit_bytes=58 * 1024 * 1024)


def project_up(tokens, gate, up, gate_scale, up_scale):
    count, model = tokens.shape
    words, width = gate.shape
    groups = gate_scale.shape[0]
    tile = tile_of(width, 512)
    codes = pl.BlockSpec((words, tile), lambda i: (0, i))
    scales = pl.BlockSpec((groups, tile), lambda i: (0, i))
    return pl.pallas_call(
        up_kernel,
        grid=(width // tile,),
        in_specs=[pl.BlockSpec((count, model), lambda i: (0, 0)), codes, codes, scales, scales],
        out_specs=pl.BlockSpec((2, count, tile), lambda i: (0, 0, i)),
        out_shape=jax.ShapeDtypeStruct((2, count, width), jnp.bfloat16),
        scratch_shapes=[
            pltpu.VMEM((count, model), jnp.bfloat16),
            pltpu.VMEM((2, model, tile), jnp.bfloat16),
        ],
        cost_estimate=pl.CostEstimate(
            flops=4 * count * model * width,
            bytes_accessed=8 * words * width,
            transcendentals=0,
        ),
        compiler_params=pltpu.CompilerParams(**PARAMS),
    )(tokens, gate, up, gate_scale, up_scale)


def project_down(hidden, codes, scale):
    count, units = hidden.shape
    words, width = codes.shape
    groups = scale.shape[0]
    tile = tile_of(width, 512)
    return pl.pallas_call(
        down_kernel,
        grid=(width // tile,),
        in_specs=[
            pl.BlockSpec((count, units), lambda i: (0, 0)),
            pl.BlockSpec((words, tile), lambda i: (0, i)),
            pl.BlockSpec((groups, tile), lambda i: (0, i)),
        ],
        out_specs=pl.BlockSpec((count, tile), lambda i: (0, i)),
        out_shape=jax.ShapeDtypeStruct((count, width), jnp.bfloat16),
        scratch_shapes=[
            pltpu.VMEM((count, units), jnp.bfloat16),
            pltpu.VMEM((units, tile), jnp.bfloat16),
        ],
        cost_estimate=pl.CostEstimate(
            flops=2 * count * units * width,
            bytes_accessed=4 * words * width,
            transcendentals=0,
        ),
        compiler_params=pltpu.CompilerParams(**PARAMS),
    )(hidden, codes, scale)


VMEM_REF = pl.BlockSpec(memory_space=pltpu.VMEM)
MESH = pl.DeviceIdType.MESH
DMA = pltpu.SemaphoreType.DMA
REMOTE = pltpu.CompilerParams(has_side_effects=True, vmem_limit_bytes=58 * 1024 * 1024)


def gather_kernel(
    rows, cols, share, tokens, gate, up, down, all_tokens, gate_out, up_out, down_out,
    gate_got, up_got, down_got, token_send, token_recv, scale_send, scale_recv,
):
    row, col = lax.axis_index("row"), lax.axis_index("col")
    count, width = tokens.shape[0], gate_got.shape[2]
    home, slot = lax.div(row, share), lax.rem(row, share)
    group = lax.rem(col - home + cols, cols)
    sibling = row + 1 - 2 * lax.rem(row, 2)

    def block(owner):
        return pl.ds(pl.multiple_of(owner * count, count), count)

    def token_copy(step, peer, source, owner):
        return pltpu.make_async_remote_copy(
            src_ref=source,
            dst_ref=all_tokens.at[block(owner)],
            send_sem=token_send.at[step],
            recv_sem=token_recv.at[step],
            device_id={"row": peer, "col": col},
            device_id_type=MESH,
        )

    def own(step):
        return token_copy(step, lax.rem(row + step, rows), tokens, row)

    def relay(step):
        owner = lax.rem(row - step + rows, rows)
        return token_copy(step + 1, sibling, all_tokens.at[block(owner)], owner)

    to_sibling = token_copy(1, sibling, tokens, row)

    def scale_copies(j, at, peer_row, peer_col):
        columns = pl.ds(pl.multiple_of((group * share + j) * width, 128), width)
        pairs = (
            (gate.at[:, columns], gate_got.at[at]),
            (up.at[:, columns], up_got.at[at]),
            (down.at[group * share + j], down_got.at[at]),
        )
        return pairs, [
            pltpu.make_async_remote_copy(
                src_ref=source,
                dst_ref=target,
                send_sem=scale_send.at[kind, j],
                recv_sem=scale_recv.at[kind, at],
                device_id={"row": peer_row, "col": peer_col},
                device_id_type=MESH,
            )
            for kind, (source, target) in enumerate(pairs)
        ]

    for j in range(share):
        peer = group * share + j
        pairs, copies = scale_copies(j, slot, peer, home)
        here = jnp.logical_and(peer == row, home == col)

        @pl.when(jnp.logical_not(here))
        def _():
            for copy in copies:
                copy.start()

        @pl.when(here)
        def _():
            for source, target in pairs:
                target[...] = source[...]

    for step in range(rows - 2, 0, -2):
        own(step).start()
    to_sibling.start()
    all_tokens[block(row)] = tokens[...]
    for step in range(rows - 2, 0, -2):
        own(step).wait_recv()
        relay(step).start()

    other = lax.rem(row + 1, rows)
    from_col = lax.rem(col + lax.div(row, share), cols)
    for t in range(share):
        @pl.when(jnp.logical_or(col * share + t != row, from_col != col))
        def _():
            for copy in scale_copies(0, t, other, col)[1]:
                copy.wait_recv()

    lines, span = gate_got.shape[1], down_got.shape[2]
    for t in range(share):
        gate_out[t * lines : (t + 1) * lines] = gate_got[t].astype(jnp.float32)
        up_out[t * lines : (t + 1) * lines] = up_got[t].astype(jnp.float32)
        down_out[:, t * span : (t + 1) * span] = down_got[t].astype(jnp.float32)
    to_sibling.wait()
    for step in range(2, rows, 2):
        own(step).wait_send()
        relay(step).wait()
    for j in range(share):
        peer = group * share + j

        @pl.when(jnp.logical_not(jnp.logical_and(peer == row, home == col)))
        def _():
            for copy in scale_copies(j, slot, peer, home)[1]:
                copy.wait_send()


def gather(tokens, gate, up, down, rows, cols):
    count, model = tokens.shape
    lines = gate.shape[0]
    width = gate.shape[1] // rows
    groups, span = down.shape[0] // rows, down.shape[1]
    share = rows // cols
    down = down.reshape(rows, groups, span)
    return pl.pallas_call(
        functools.partial(gather_kernel, rows, cols, share),
        in_specs=[VMEM_REF] * 4,
        out_specs=[VMEM_REF] * 4,
        out_shape=[
            jax.ShapeDtypeStruct((count * rows, model), jnp.bfloat16),
            jax.ShapeDtypeStruct((share * lines, width), jnp.float32),
            jax.ShapeDtypeStruct((share * lines, width), jnp.float32),
            jax.ShapeDtypeStruct((groups, share * span), jnp.float32),
        ],
        scratch_shapes=[
            pltpu.VMEM((share, lines, width), jnp.bfloat16),
            pltpu.VMEM((share, lines, width), jnp.bfloat16),
            pltpu.VMEM((share, groups, span), jnp.bfloat16),
            DMA((rows,)),
            DMA((rows,)),
            DMA((3, share)),
            DMA((3, share)),
        ],
        compiler_params=REMOTE,
        name="gather",
    )(tokens, gate, up, down)


def chain_kernel(cols, chunks, sums, hidden, got, sum_send, sum_recv, hid_send, hid_recv):
    col = lax.axis_index("col")
    last = cols - 1
    half = sums.shape[1] // 2
    depth = half // chunks
    before, after = jnp.maximum(col - 1, 0), jnp.minimum(col + 1, last)
    any_peer = jnp.where(col == last, col - 1, col + 1)
    sides = ((last, 0, before, after), (0, last, after, before))

    def rows_of(side, q):
        return pl.ds(pl.multiple_of(side * half + q * depth, depth), depth)

    def sum_copy(side, q, source, peer):
        return pltpu.make_async_remote_copy(
            src_ref=source,
            dst_ref=got.at[side, q],
            send_sem=sum_send.at[side, q],
            recv_sem=sum_recv.at[side, q],
            device_id={"col": peer},
            device_id_type=MESH,
        )

    def hid_copy(side, q, peer):
        return pltpu.make_async_remote_copy(
            src_ref=hidden.at[rows_of(side, q)],
            dst_ref=hidden.at[rows_of(side, q)],
            send_sem=hid_send.at[side, q],
            recv_sem=hid_recv.at[side, q],
            device_id={"col": peer},
            device_id_type=MESH,
        )

    for side, (first, end, down_peer, up_peer) in enumerate(sides):
        @pl.when(col == first)
        def _():
            for q in range(chunks):
                sum_copy(side, q, sums.at[:, rows_of(side, q)], down_peer).start()

    def sum_step(step, carry):
        for side, (first, end, down_peer, up_peer) in enumerate(sides):
            q = step - (jnp.abs(col - first) - 1)

            @pl.when((col != first) & (q >= 0) & (q < chunks))
            def _():
                sum_copy(side, q, got.at[side, q], any_peer).wait_recv()
                total = got[side, q].astype(jnp.float32) + sums[:, rows_of(side, q)].astype(
                    jnp.float32
                )

                @pl.when(col != end)
                def _():
                    got[side, q] = total.astype(jnp.bfloat16)
                    sum_copy(side, q, got.at[side, q], down_peer).start()

                @pl.when(col == end)
                def _():
                    value = jax.nn.silu(total[0]) * total[1]
                    hidden[rows_of(side, q)] = value.astype(jnp.bfloat16)
                    hid_copy(side, q, up_peer).start()
        return carry

    def hid_step(step, carry):
        for side, (first, end, down_peer, up_peer) in enumerate(sides):
            q = step - (jnp.abs(col - end) - 1)

            @pl.when((col != end) & (q >= 0) & (q < chunks))
            def _():
                hid_copy(side, q, any_peer).wait_recv()

                @pl.when(col != first)
                def _():
                    hid_copy(side, q, up_peer).start()
        return carry

    lax.fori_loop(0, chunks + cols - 2, sum_step, 0)
    lax.fori_loop(0, chunks + cols - 2, hid_step, 0)

    for q in range(chunks):
        for side, (first, end, down_peer, up_peer) in enumerate(sides):
            @pl.when(col != end)
            def _():
                sum_copy(side, q, got.at[side, q], any_peer).wait_send()

            @pl.when(col != first)
            def _():
                hid_copy(side, q, any_peer).wait_send()


def chain(sums, cols):
    _, count, width = sums.shape
    chunks = 8
    while count % (2 * 16 * chunks):
        chunks //= 2
    depth = count // (2 * chunks)
    return pl.pallas_call(
        functools.partial(chain_kernel, cols, chunks),
        in_specs=[VMEM_REF],
        out_specs=VMEM_REF,
        out_shape=jax.ShapeDtypeStruct((count, width), jnp.bfloat16),
        scratch_shapes=[
            pltpu.VMEM((2, chunks, 2, depth, width), jnp.bfloat16),
            DMA((2, chunks)),
            DMA((2, chunks)),
            DMA((2, chunks)),
            DMA((2, chunks)),
        ],
        compiler_params=REMOTE,
        name="chain",
    )(sums)


def scatter_kernel(rows, partial, out, got, send, recv):
    row = lax.axis_index("row")
    count = out.shape[0]

    def block(index):
        return pl.ds(pl.multiple_of(index * count, count), count)

    def copy(step):
        peer = lax.rem(row + step, rows)
        return pltpu.make_async_remote_copy(
            src_ref=partial.at[block(peer)],
            dst_ref=got.at[step - 1],
            send_sem=send.at[step - 1],
            recv_sem=recv.at[step - 1],
            device_id={"row": peer},
            device_id_type=MESH,
        )

    for step in range(rows - 1, 0, -1):
        copy(step).start()
    total = partial[block(row)].astype(jnp.float32)
    for step in range(rows - 1, 0, -1):
        copy(step).wait_recv()
        total = total + got[step - 1].astype(jnp.float32)
    out[...] = total.astype(jnp.bfloat16)
    for step in range(1, rows):
        copy(step).wait_send()


def scatter(partial, rows):
    count, width = partial.shape
    return pl.pallas_call(
        functools.partial(scatter_kernel, rows),
        in_specs=[VMEM_REF],
        out_specs=VMEM_REF,
        out_shape=jax.ShapeDtypeStruct((count // rows, width), jnp.bfloat16),
        scratch_shapes=[
            pltpu.VMEM((rows - 1, count // rows, width), jnp.bfloat16),
            DMA((rows - 1,)),
            DMA((rows - 1,)),
        ],
        compiler_params=REMOTE,
        name="scatter",
    )(partial)


def per_device(tokens, gate_codes, up_codes, down_codes, gate_scales, up_scales, down_scales):
    rows, cols = lax.axis_size("row"), lax.axis_size("col")
    gathered, gate_part, up_part, down_part = gather(
        tokens, gate_scales, up_scales, down_scales.T, rows, cols
    )
    sums = project_up(gathered, gate_codes, up_codes, gate_part, up_part)
    hidden = chain(sums, cols)
    return scatter(project_down(hidden, down_codes, down_part), rows)


def solution(mesh):
    placed = (
        P("row", "col"),
        P("col", "row"),
        P("col", "row"),
        P("row", "col"),
        P("row", None),
        P("row", None),
        P("row", None),
    )
    return jax.shard_map(
        per_device, mesh=mesh, in_specs=placed, out_specs=P("row", "col"), check_vma=False
    )
```

profile of v0, /device:TPU:0, one launch (start us, length us, event | category | flops | bytes accessed | tf_op | source)
XLA Modules:
  0.0 182.4 jit_solution(17437046346400138819)
XLA Ops:
  0.0 1.9 %reshape.3.down = bf16[8,28,1024]{2,1,0:T(8,128)(2,1)} reshape(bf16[224,1024]{1,0:T(8,128)(2,1)} %bitcast.1) | data formatting | bytes 917504 | tf_op jit(solution)/shard_map/reshape | solution.py:243
  1.9 25.2 %gather.1 = (bf16[256,2048]{1,0:T(8,128)(2,1)}, f32[16,3584]{1,0:T(8,128)}, f32[16,3584]{1,0:T(8,128)}, f32[28,2048]{1,0:T(8,128)}) custom-call(bf16[32,2048]{1,0:T(8,128)(2,1)} %tokens.1, bf16[8,28672]{1,0:T(8,128)(2,1)} %gate.2, bf16[8,28672]{1,0:T(8,128)(2,1)} %up.2, bf16[8,28,1024]{2,1,0:T(8,128)(2,1)} %reshape.3.down), custom_call_target="tpu_custom_call" | custom-call | tf_op jit(solution)/shard_map/gather/pallas_call | solution.py:244
  27.1 23.7 %shard_map.73.sums = bf16[2,256,3584]{2,1,0:T(8,128)(2,1)} custom-call(bf16[256,2048]{1,0:T(8,128)(2,1)} %get-tuple-element.9.tokens, s32[256,3584]{1,0:T(8,128)} %gate.3, s32[256,3584]{1,0:T(8,128)} %up.3, f32[16,3584]{1,0:T(8,128)} %get-tuple-element.10.gate_scale, f32[16,3584]{1,0:T(8,128)} %get-tuple-element.11.up_scale), custom_call_target="tpu_custom_call" | custom-call | flops 7516192768 | bytes 7340032 | tf_op jit(solution)/shard_map/pallas_call | solution.py:84
  50.8 97.4 %chain.1.hidden = bf16[256,3584]{1,0:T(8,128)(2,1)} custom-call(bf16[2,256,3584]{2,1,0:T(8,128)(2,1)} %shard_map.73.sums), custom_call_target="tpu_custom_call" | custom-call | tf_op jit(solution)/shard_map/chain/pallas_call | solution.py:362
  148.2 13.0 %shard_map.74.partial = bf16[256,2048]{1,0:T(8,128)(2,1)} custom-call(bf16[256,3584]{1,0:T(8,128)(2,1)} %chain.1.hidden, s32[448,2048]{1,0:T(8,128)} %codes.1, f32[28,2048]{1,0:T(8,128)} %get-tuple-element.12.scale), custom_call_target="tpu_custom_call" | custom-call | flops 3758096384 | bytes 3670016 | tf_op jit(solution)/shard_map/pallas_call | solution.py:108
  161.2 19.6 %scatter.1 = bf16[32,2048]{1,0:T(8,128)(2,1)} custom-call(bf16[256,2048]{1,0:T(8,128)(2,1)} %shard_map.74.partial), custom_call_target="tpu_custom_call" | custom-call | tf_op jit(solution)/shard_map/scatter/pallas_call | solution.py:410
  180.8 1.6 copy.9
where the time goes:
time: 183 us; the launch traced here: 182 us
  Pallas kernels  179 us (98%)
  local copies, waits for them, and re-layouts  3.46 us (2%)
    pallas_call x1, Pallas kernels, chain(): pl.pallas_call(functools.partial(chain_kernel, cols, chunks), in_specs=[V...  97.4 us
    pallas_call x1, Pallas kernels, gather(): pl.pallas_call(functools.partial(gather_kernel, rows, cols, share), in_sp...  25.2 us
    pallas_call x1, Pallas kernels, project_up(): pl.pallas_call(up_kernel, grid=(width // tile,), in_specs=[pl.BlockSpec((...  23.7 us
    pallas_call x1, Pallas kernels, scatter(): pl.pallas_call(functools.partial(scatter_kernel, rows), in_specs=[VMEM_RE...  19.6 us
    pallas_call x1, Pallas kernels, project_down(): pl.pallas_call(down_kernel, grid=(width // tile,), in_specs=[pl.BlockSpec...  13 us

commit v1 on v0

v1 whole, which is shorter than its diff:
```python
import functools

import jax
import jax.numpy as jnp
from jax import lax
from jax.experimental import pallas as pl
from jax.experimental.pallas import tpu as pltpu
from jax.sharding import PartitionSpec as P

GROUP = 128
PACK = 8
SUB = GROUP // PACK
MESH = pl.DeviceIdType.MESH
DMA = pltpu.SemaphoreType.DMA
S_LAG = 2
H_LAG = 2
FLIP = -2004318072


def permutation():
    source = lax.broadcasted_iota(jnp.int32, (GROUP, GROUP), 0)
    target = lax.broadcasted_iota(jnp.int32, (GROUP, GROUP), 1)
    wanted = lax.rem(target, SUB) * PACK + lax.div(target, SUB)
    return (source == wanted).astype(jnp.bfloat16)


def pieces_of(chunks):
    bounds = sorted({0, max(1, chunks // 7), max(1, 3 * chunks // 7), chunks})
    return list(zip(bounds[:-1], bounds[1:]))


def nibbles(word, k):
    code = word if k == PACK - 1 else jnp.left_shift(word, 28 - 4 * k)
    return jnp.right_shift(code, 28).astype(jnp.float32)


def layer_kernel(
    rows, cols, chunks,
    tokens, gate, up, down, gate_scale, up_scale, down_scale, out,
    all_tokens, moved, gate_codes, up_codes, down_codes,
    gate_got, up_got, down_got, unit_scale, down_rows,
    dense, dense_down, sums, got, hidden, acc,
    half_send, half_got, comb, final_got,
    local_sem, token_send, token_recv, relay_send, relay_recv,
    scale_send, scale_recv, down_send, down_recv,
    sum_send, sum_recv, hid_send, hid_recv,
    half_ssem, half_rsem, final_ssem, final_rsem,
):
    row, col = lax.axis_index("row"), lax.axis_index("col")
    core = lax.rem(row, 2)
    chip = row - core
    sibling = row + 1 - 2 * core
    chips = rows // 2
    share = rows // cols
    last = cols - 1
    count, model = tokens.shape
    total_tokens = count * rows
    half = total_tokens // 2
    width = gate.shape[1]
    lines = gate_scale.shape[0]
    groups = share * lines
    pair = 2 if chunks % 2 == 0 else 1
    pieces = pieces_of(chunks)
    home = lax.div(row, share) == col
    slot = lax.rem(row, share)
    exact = chips & (chips - 1) == 0

    def other(j):
        if not exact:
            return lax.rem(chip + 2 * j, rows)
        peer, bit = chip, 2
        while bit <= 2 * j:
            if (2 * j) & bit:
                peer = peer + bit - 2 * bit * lax.rem(lax.div(chip, bit), 2)
            bit *= 2
        return peer

    def back(j):
        return j if exact else (chips - j) % chips

    def block(side, j):
        return pl.ds(pl.multiple_of((side * chips + j) * count, count), count)

    def remote(source, target, send, recv, **where):
        return pltpu.make_async_remote_copy(
            src_ref=source, dst_ref=target, send_sem=send, recv_sem=recv,
            device_id=where, device_id_type=MESH,
        )

    own_copy = pltpu.make_async_copy(tokens, all_tokens.at[block(core, 0)], local_sem.at[0])
    own_copy.start()

    def code_copies(i):
        first, end = pieces[i]
        at = pl.ds(first * GROUP, (end - first) * GROUP)
        return [
            pltpu.make_async_copy(gate.at[:, at], gate_codes.at[:, at], local_sem.at[2 + 2 * i]),
            pltpu.make_async_copy(up.at[:, at], up_codes.at[:, at], local_sem.at[3 + 2 * i]),
        ]

    for copy in code_copies(0):
        copy.start()

    barrier = pltpu.get_barrier_semaphore()
    for step in range(1, rows):
        pl.semaphore_signal(
            barrier, inc=1, device_id={"row": lax.rem(row + step, rows)}, device_id_type=MESH
        )

    @pl.when(col > 0)
    def _():
        pl.semaphore_signal(barrier, inc=1, device_id={"col": col - 1}, device_id_type=MESH)

    @pl.when(col < last)
    def _():
        pl.semaphore_signal(barrier, inc=1, device_id={"col": col + 1}, device_id_type=MESH)

    inner = jnp.logical_and(col > 0, col < last)

    @pl.when(inner)
    def _():
        pl.semaphore_wait(barrier, rows + 1)

    @pl.when(jnp.logical_not(inner))
    def _():
        pl.semaphore_wait(barrier, rows)

    def scale_copy(kind, i, step):
        first, end = pieces[i]
        peer = lax.rem(row + step, rows)
        span = (end - first) * GROUP
        source, target = ((gate_scale, gate_got), (up_scale, up_got))[kind]
        source = source.at[:, pl.ds(pl.multiple_of(peer * width + first * GROUP, GROUP), span)]
        target = target.at[slot, :, pl.ds(first * GROUP, span)]
        if step == 0:
            return pltpu.make_async_copy(source, target, scale_recv.at[kind, i, slot])
        return remote(
            source, target, scale_send.at[kind, i, step], scale_recv.at[kind, i, slot], row=peer
        )

    def down_copy(step):
        peer = lax.rem(row + step, rows)
        if step == 0:
            return pltpu.make_async_copy(
                down_scale.at[peer], down_got.at[slot], down_recv.at[slot]
            )
        return remote(
            down_scale.at[peer], down_got.at[slot], down_send.at[step], down_recv.at[slot], row=peer
        )

    def start_scales(i):
        @pl.when(home)
        def _():
            for step in range(rows):
                for kind in range(2):
                    scale_copy(kind, i, step).start()

    def wait_slot(copy_of, t, finish):
        here = row == col * share + t

        @pl.when(here)
        def _():
            copy_of(0).wait()

        @pl.when(jnp.logical_not(here))
        def _():
            finish().wait_recv()

    def wait_scales(i):
        first, end = pieces[i]
        at = pl.ds(first * GROUP, (end - first) * GROUP)
        peer = lax.rem(row + 1, rows)
        for t in range(share):
            for kind, target in enumerate((gate_got, up_got)):
                source = (gate_scale, up_scale)[kind]
                wait_slot(
                    lambda step: scale_copy(kind, i, step),
                    t,
                    lambda: remote(
                        source.at[:, at], target.at[t, :, at], scale_send.at[kind, i, 1],
                        scale_recv.at[kind, i, t], row=peer,
                    ),
                )

    def wait_down():
        peer = lax.rem(row + 1, rows)
        span = down_got.shape[2]
        for t in range(share):
            wait_slot(
                down_copy,
                t,
                lambda: remote(
                    down_scale.at[0], down_got.at[t], down_send.at[1], down_recv.at[t], row=peer
                ),
            )
        for t in range(share):
            down_rows[:, t * span : (t + 1) * span] = down_got[t].astype(jnp.float32)

    def token_copy(j, target):
        return remote(
            all_tokens.at[block(core, 0)], all_tokens.at[block(core, target)],
            token_send.at[j], token_recv.at[target], row=other(j) + core,
        )

    def relay(j):
        return remote(
            all_tokens.at[block(core, j)], all_tokens.at[block(core, j)],
            relay_send.at[j], relay_recv.at[j], row=sibling,
        )

    start_scales(0)
    own_copy.wait()
    for j in range(chips - 1, 0, -1):
        token_copy(j, back(j)).start()
    relay(0).start()
    for i in range(1, len(pieces)):
        start_scales(i)
        for copy in code_copies(i):
            copy.start()

    @pl.when(home)
    def _():
        for step in range(rows):
            down_copy(step).start()

    down_load = pltpu.make_async_copy(down, down_codes, local_sem.at[1])
    down_load.start()
    acc[...] = jnp.zeros_like(acc)
    for j in range(1, chips):
        token_copy(back(j), j).wait_recv()
        relay(j).start()
    for j in range(chips):
        relay(j).wait_recv()

    rows_step = min(total_tokens, 256)
    perm = permutation()

    def permute(i, carry):
        lines_at = pl.ds(pl.multiple_of(i * rows_step, rows_step), rows_step)
        for group in range(model // GROUP):
            at = pl.ds(group * GROUP, GROUP)
            moved[lines_at, at] = jnp.dot(
                all_tokens[lines_at, at], perm, preferred_element_type=jnp.float32
            ).astype(jnp.bfloat16)
        return carry

    lax.fori_loop(0, total_tokens // rows_step, permute, 0)

    batch = 4 if groups % 4 == 0 else 1

    def compute(t):
        at = pl.ds(pl.multiple_of(t * GROUP, GROUP), GROUP)
        for kind, (codes, scale) in enumerate(((gate_codes, gate_got), (up_codes, up_got))):
            for s in range(share):
                unit_scale[kind, s * lines : (s + 1) * lines, :] = scale[s, :, at].astype(jnp.float32)

        def one(b, carry):
            for kind, codes in enumerate((gate_codes, up_codes)):
                word = codes[pl.ds(pl.multiple_of(b * batch * SUB, SUB), batch * SUB), at] ^ FLIP
                word = word.reshape(batch, SUB, GROUP)
                scale = jnp.stack(
                    [unit_scale[kind, pl.ds(b * batch + i, 1), :] for i in range(batch)]
                )
                for k in range(PACK):
                    value = (nibbles(word, k) * scale).astype(jnp.bfloat16)
                    dense[pl.ds(b * batch, batch), k, :, kind * GROUP : (kind + 1) * GROUP] = value
            return carry

        lax.fori_loop(0, groups // batch, one, 0)

        def multiply(i, carry):
            lines_at = pl.ds(pl.multiple_of(i * rows_step, rows_step), rows_step)
            total = jnp.dot(
                moved[lines_at, :],
                dense[...].reshape(model, 2 * GROUP),
                preferred_element_type=jnp.float32,
            )
            sums[t, lines_at, :] = total.astype(jnp.bfloat16)
            return carry

        lax.fori_loop(0, total_tokens // rows_step, multiply, 0)

    def side_rows(side):
        return pl.ds(side * half, half)

    def sum_copy(side, q, source, peer):
        return remote(
            source, got.at[side, q], sum_send.at[side, q], sum_recv.at[side, q], col=peer
        )

    def hid_copy(side, q, peer):
        ref = hidden.at[q, side_rows(side)]
        return remote(ref, ref, hid_send.at[side, q], hid_recv.at[side, q], col=peer)

    before, after = jnp.maximum(col - 1, 0), jnp.minimum(col + 1, last)
    any_peer = jnp.where(col == last, col - 1, col + 1)
    sides = ((col, after, before), (last - col, before, after))

    def dequantize_down(p):
        for i in range(pair):
            group = p * pair + i
            word = down_codes[pl.ds(pl.multiple_of(group * SUB, SUB), SUB), :] ^ FLIP
            scale = down_rows[pl.ds(group, 1), :]
            for k in range(PACK):
                dense_down[i, k] = (nibbles(word, k) * scale).astype(jnp.bfloat16)

    columns = 512 if model % 512 == 0 else GROUP

    def multiply_down(p):
        def one(i, carry):
            lines_at = pl.ds(pl.multiple_of(i * rows_step, rows_step), rows_step)
            left = jnp.concatenate(
                [hidden[p * pair + c, lines_at, :] for c in range(pair)], axis=1
            )
            for n in range(0, model, columns):
                at = pl.ds(n, columns)
                acc[lines_at, at] += jnp.dot(
                    left,
                    dense_down[:, :, :, at].reshape(pair * GROUP, columns),
                    preferred_element_type=jnp.float32,
                )
            return carry

        lax.fori_loop(0, total_tokens // rows_step, one, 0)

    drain = last * (S_LAG + H_LAG)

    def tick(t, carry):
        for i, (first, end) in enumerate(pieces):
            @pl.when(t == first)
            def _():
                for copy in code_copies(i):
                    copy.wait()
                wait_scales(i)

        @pl.when(t < chunks)
        def _():
            compute(t)
            for side, (hops, onward, backward) in enumerate(sides):
                @pl.when(hops == 0)
                def _():
                    sum_copy(side, t, sums.at[t, side_rows(side)], onward).start()

        for side, (hops, onward, backward) in enumerate(sides):
            q = t - S_LAG * hops

            @pl.when((hops > 0) & (q >= 0) & (q < chunks))
            def _():
                sum_copy(side, q, got.at[side, q], any_peer).wait_recv()
                total = got[side, q].astype(jnp.float32) + sums[
                    q, side_rows(side), :
                ].astype(jnp.float32)

                @pl.when(hops < last)
                def _():
                    got[side, q] = total.astype(jnp.bfloat16)
                    sum_copy(side, q, got.at[side, q], onward).start()

                @pl.when(hops == last)
                def _():
                    value = jax.nn.silu(total[:, :GROUP]) * total[:, GROUP:]
                    hidden[q, side_rows(side), :] = jnp.dot(
                        value.astype(jnp.bfloat16), perm, preferred_element_type=jnp.float32
                    ).astype(jnp.bfloat16)
                    hid_copy(side, q, backward).start()

        done = t - drain
        active = jnp.logical_and(done >= 0, lax.rem(done + pair, pair) == pair - 1)

        @pl.when(done == 0)
        def _():
            down_load.wait()
            wait_down()

        @pl.when(active)
        def _():
            dequantize_down(lax.div(done, pair))

        for side, (hops, onward, backward) in enumerate(sides):
            left = last - hops
            q = t - S_LAG * last - H_LAG * left

            @pl.when((left > 0) & (q >= 0) & (q < chunks))
            def _():
                hid_copy(side, q, any_peer).wait_recv()

                @pl.when(left < last)
                def _():
                    hid_copy(side, q, backward).start()

        @pl.when(active)
        def _():
            multiply_down(lax.div(done, pair))

        return carry

    lax.fori_loop(0, chunks + drain, tick, 0)

    def half_copy(j):
        return remote(
            half_send.at[j], half_got.at[j], half_ssem.at[j], half_rsem.at[j], row=sibling
        )

    def final_copy(j, target):
        return remote(
            comb.at[j], final_got.at[target], final_ssem.at[j], final_rsem.at[target],
            row=other(j) + core,
        )

    for j in range(chips - 1, -1, -1):
        half_send[j] = acc[block(1 - core, j), :].astype(jnp.bfloat16)
        half_copy(j).start()
    for j in range(chips - 1, 0, -1):
        half_copy(j).wait_recv()
        comb[j] = (acc[block(core, j), :] + half_got[j].astype(jnp.float32)).astype(jnp.bfloat16)
        final_copy(j, back(j)).start()
    half_copy(0).wait_recv()
    total = acc[block(core, 0), :] + half_got[0].astype(jnp.float32)
    for j in range(1, chips):
        final_copy(back(j), j).wait_recv()
        total = total + final_got[j].astype(jnp.float32)
    out[...] = total.astype(jnp.bfloat16)

    for j in range(1, chips):
        token_copy(j, back(j)).wait_send()
        final_copy(j, back(j)).wait_send()
    for j in range(chips):
        relay(j).wait_send()
        half_copy(j).wait_send()

    @pl.when(home)
    def _():
        for step in range(1, rows):
            for i in range(len(pieces)):
                for kind in range(2):
                    scale_copy(kind, i, step).wait_send()
            down_copy(step).wait_send()

    def sent(q, carry):
        for side, (hops, onward, backward) in enumerate(sides):
            @pl.when(hops < last)
            def _():
                sum_copy(side, q, got.at[side, q], any_peer).wait_send()

            @pl.when(hops > 0)
            def _():
                hid_copy(side, q, any_peer).wait_send()

        return carry

    lax.fori_loop(0, chunks, sent, 0)


def layer(tokens, gate, up, down, gate_scale, up_scale, down_scale, rows, cols):
    count, model = tokens.shape
    words, width = gate.shape
    lines = gate_scale.shape[0]
    share = rows // cols
    down_groups = down_scale.shape[1] // rows
    span = down_scale.shape[0]
    down_scale = down_scale.T.reshape(rows, down_groups, span)
    chunks = width // GROUP
    chips = rows // 2
    tokens_all = count * rows
    half = tokens_all // 2
    groups = share * lines
    pair = 2 if chunks % 2 == 0 else 1
    parts = len(pieces_of(chunks))
    any_spec = pl.BlockSpec(memory_space=pl.ANY)
    bf16, f32, i32 = jnp.bfloat16, jnp.float32, jnp.int32
    return pl.pallas_call(
        functools.partial(layer_kernel, rows, cols, chunks),
        in_specs=[any_spec] * 7,
        out_specs=pl.BlockSpec(memory_space=pltpu.VMEM),
        out_shape=jax.ShapeDtypeStruct((count, model), bf16),
        scratch_shapes=[
            pltpu.VMEM((tokens_all, model), bf16),
            pltpu.VMEM((tokens_all, model), bf16),
            pltpu.VMEM((words, width), i32),
            pltpu.VMEM((words, width), i32),
            pltpu.VMEM(down.shape, i32),
            pltpu.VMEM((share, lines, width), bf16),
            pltpu.VMEM((share, lines, width), bf16),
            pltpu.VMEM((share, down_groups, span), bf16),
            pltpu.VMEM((2, groups, GROUP), f32),
            pltpu.VMEM((down_groups, share * span), f32),
            pltpu.VMEM((groups, PACK, SUB, 2 * GROUP), bf16),
            pltpu.VMEM((pair, PACK, SUB, model), bf16),
            pltpu.VMEM((chunks, tokens_all, 2 * GROUP), bf16),
            pltpu.VMEM((2, chunks, half, 2 * GROUP), bf16),
            pltpu.VMEM((chunks, tokens_all, GROUP), bf16),
            pltpu.VMEM((tokens_all, model), f32),
            pltpu.VMEM((chips, count, model), bf16),
            pltpu.VMEM((chips, count, model), bf16),
            pltpu.VMEM((chips, count, model), bf16),
            pltpu.VMEM((chips, count, model), bf16),
            DMA((2 + 2 * parts,)),
            DMA((chips,)),
            DMA((chips,)),
            DMA((chips,)),
            DMA((chips,)),
            DMA((2, parts, rows)),
            DMA((2, parts, share)),
            DMA((rows,)),
            DMA((share,)),
            DMA((2, chunks)),
            DMA((2, chunks)),
            DMA((2, chunks)),
            DMA((2, chunks)),
            DMA((chips,)),
            DMA((chips,)),
            DMA((chips,)),
            DMA((chips,)),
        ],
        compiler_params=pltpu.CompilerParams(
            collective_id=0, has_side_effects=True, vmem_limit_bytes=60 * 1024 * 1024
        ),
        name="layer",
    )(tokens, gate, up, down, gate_scale, up_scale, down_scale)


def per_device(tokens, gate_codes, up_codes, down_codes, gate_scales, up_scales, down_scales):
    rows, cols = lax.axis_size("row"), lax.axis_size("col")
    return layer(
        tokens, gate_codes, up_codes, down_codes, gate_scales, up_scales, down_scales, rows, cols
    )


def solution(mesh):
    placed = (
        P("row", "col"),
        P("col", "row"),
        P("col", "row"),
        P("row", "col"),
        P("row", None),
        P("row", None),
        P("row", None),
    )
    return jax.shard_map(
        per_device, mesh=mesh, in_specs=placed, out_specs=P("row", "col"), check_vma=False
    )
```

time: 183 us -> 106 us (0.58)
  Pallas kernels: 179 us -> 102 us
    pallas_call x5 -> x1, Pallas kernels: 179 us -> 102 us  [layer(): pl.pallas_call(functools.partial(layer_kernel, rows, cols, chunks), in_sp...]
where the time goes in v1:
time: 106 us
  Pallas kernels  102 us (96%)
  local copies, waits for them, and re-layouts  3.46 us (3%)
    pallas_call x1, Pallas kernels, layer(): pl.pallas_call(functools.partial(layer_kernel, rows, cols, chunks), in_sp...  102 us

profile of v1, /device:TPU:0, one launch (start us, length us, event | category | flops | bytes accessed | tf_op | source)
XLA Modules:
  0.0 105.6 jit_solution(4533127512953139025)
XLA Ops:
  0.0 1.9 %reshape.3.down_scale = bf16[8,28,1024]{2,1,0:T(8,128)(2,1)} reshape(bf16[224,1024]{1,0:T(8,128)(2,1)} %bitcast.1) | data formatting | bytes 917504 | tf_op jit(solution)/shard_map/reshape | solution.py:461
  1.9 102.1 %layer.1 = bf16[32,2048]{1,0:T(8,128)(2,1)} custom-call(bf16[32,2048]{1,0:T(8,128)(2,1)} %tokens.1, s32[256,3584]{1,0:T(8,128)} %gate.1, s32[256,3584]{1,0:T(8,128)} %up.1, s32[448,2048]{1,0:T(8,128)} %down.1, bf16[8,28672]{1,0:T(8,128)(2,1)} %gate_scale.1, bf16[8,28672]{1,0:T(8,128)(2,1)} %up_scale.1, bf16[8,28,1024]{2,1,0:T(8,128)(2,1)} %reshape.3.down_scale), custom_call_target="tpu_custom_call" | custom-call | tf_op jit(solution)/shard_map/layer/pallas_call | solution.py:471
  104.0 1.6 %copy.9 = bf16[32,2048]{1,0:T(8,128)(2,1)} copy(bf16[32,2048]{1,0:T(8,128)(2,1)} %layer.1) | data formatting | bytes 262144

commit v2 on v1

--- a/solution.py
+++ b/solution.py
@@ -12,8 +12,9 @@
 SUB = GROUP // PACK
 MESH = pl.DeviceIdType.MESH
 DMA = pltpu.SemaphoreType.DMA
-S_LAG = 2
-H_LAG = 2
+S_LAG = 3
+H_LAG = 3
+H_WAIT = 4
 FLIP = -2004318072
 
 
@@ -38,8 +39,9 @@
     rows, cols, chunks,
     tokens, gate, up, down, gate_scale, up_scale, down_scale, out,
     all_tokens, moved, gate_codes, up_codes, down_codes,
+    gate_own, up_own, down_own, down_turned,
     gate_got, up_got, down_got, unit_scale, down_rows,
-    dense, dense_down, sums, got, hidden, acc,
+    dense, dense_down, sums, got, hidden_far, hidden_near, acc_far, acc_near,
     half_send, half_got, comb, final_got,
     local_sem, token_send, token_recv, relay_send, relay_recv,
     scale_send, scale_recv, down_send, down_recv,
@@ -59,7 +61,8 @@
     width = gate.shape[1]
     lines = gate_scale.shape[0]
     groups = share * lines
-    pair = 2 if chunks % 2 == 0 else 1
+    far = half - count
+    pair, quad = 2 - chunks % 2, 4 if chunks % 4 == 0 else 1
     pieces = pieces_of(chunks)
     home = lax.div(row, share) == col
     slot = lax.rem(row, share)
@@ -100,6 +103,18 @@
 
     for copy in code_copies(0):
         copy.start()
+    first_code = 2 + 2 * len(pieces)
+    scale_loads = [
+        pltpu.make_async_copy(source, target, local_sem.at[first_code + i])
+        for i, (source, target) in enumerate(
+            ((gate_scale, gate_own), (up_scale, up_own), (down_scale, down_own))
+        )
+    ]
+
+    @pl.when(home)
+    def _():
+        for load in scale_loads:
+            load.start()
 
     barrier = pltpu.get_barrier_semaphore()
     for step in range(1, rows):
@@ -129,7 +144,7 @@
         first, end = pieces[i]
         peer = lax.rem(row + step, rows)
         span = (end - first) * GROUP
-        source, target = ((gate_scale, gate_got), (up_scale, up_got))[kind]
+        source, target = ((gate_own, gate_got), (up_own, up_got))[kind]
         source = source.at[:, pl.ds(pl.multiple_of(peer * width + first * GROUP, GROUP), span)]
         target = target.at[slot, :, pl.ds(first * GROUP, span)]
         if step == 0:
@@ -142,10 +157,10 @@
         peer = lax.rem(row + step, rows)
         if step == 0:
             return pltpu.make_async_copy(
-                down_scale.at[peer], down_got.at[slot], down_recv.at[slot]
+                down_turned.at[peer], down_got.at[slot], down_recv.at[slot]
             )
         return remote(
-            down_scale.at[peer], down_got.at[slot], down_send.at[step], down_recv.at[slot], row=peer
+            down_turned.at[peer], down_got.at[slot], down_send.at[step], down_recv.at[slot], row=peer
         )
 
     def start_scales(i):
@@ -172,7 +187,7 @@
         peer = lax.rem(row + 1, rows)
         for t in range(share):
             for kind, target in enumerate((gate_got, up_got)):
-                source = (gate_scale, up_scale)[kind]
+                source = (gate_own, up_own)[kind]
                 wait_slot(
                     lambda step: scale_copy(kind, i, step),
                     t,
@@ -190,7 +205,7 @@
                 down_copy,
                 t,
                 lambda: remote(
-                    down_scale.at[0], down_got.at[t], down_send.at[1], down_recv.at[t], row=peer
+                    down_turned.at[0], down_got.at[t], down_send.at[1], down_recv.at[t], row=peer
                 ),
             )
         for t in range(share):
@@ -207,6 +222,11 @@
             all_tokens.at[block(core, j)], all_tokens.at[block(core, j)],
             relay_send.at[j], relay_recv.at[j], row=sibling,
         )
+
+    @pl.when(home)
+    def _():
+        for load in scale_loads:
+            load.wait()
 
     start_scales(0)
     own_copy.wait()
@@ -220,12 +240,24 @@
 
     @pl.when(home)
     def _():
+        down_groups = down_own.shape[1] // rows
+        line = lax.broadcasted_iota(jnp.int32, (rows * down_got.shape[1], down_own.shape[1]), 0)
+        wanted = lax.broadcasted_iota(jnp.int32, line.shape, 1)
+        owner = lax.div(line, down_got.shape[1])
+        group = lax.rem(line, down_got.shape[1])
+        pick = (wanted == owner * down_groups + group) & (group < down_groups)
+        turned = lax.dot_general(
+            pick.astype(jnp.bfloat16), down_own[...], (((1,), (1,)), ((), ())),
+            preferred_element_type=jnp.float32,
+        )
+        down_turned[...] = turned.astype(jnp.bfloat16).reshape(down_turned.shape)
         for step in range(rows):
             down_copy(step).start()
 
     down_load = pltpu.make_async_copy(down, down_codes, local_sem.at[1])
     down_load.start()
-    acc[...] = jnp.zeros_like(acc)
+    acc_far[...] = jnp.zeros_like(acc_far)
+    acc_near[...] = jnp.zeros_like(acc_near)
     for j in range(1, chips):
         token_copy(back(j), j).wait_recv()
         relay(j).start()
@@ -288,42 +320,75 @@
             source, got.at[side, q], sum_send.at[side, q], sum_recv.at[side, q], col=peer
         )
 
-    def hid_copy(side, q, peer):
-        ref = hidden.at[q, side_rows(side)]
-        return remote(ref, ref, hid_send.at[side, q], hid_recv.at[side, q], col=peer)
+    def far_copy(side, tau, peer):
+        ref = hidden_far.at[side, pl.ds(tau * pair, pair)]
+        return remote(ref, ref, hid_send.at[side, tau], hid_recv.at[side, tau], col=peer)
+
+    def near_copy(side, tau, peer):
+        ref = hidden_near.at[side, pl.ds(tau * quad, quad)]
+        at = far_ticks + tau
+        return remote(ref, ref, hid_send.at[side, at], hid_recv.at[side, at], col=peer)
+
+    far_ticks, near_ticks = chunks // pair, chunks // quad
+    h_start = chunks + last * S_LAG - far_ticks + H_WAIT
+    d_start = h_start + last * H_LAG
 
     before, after = jnp.maximum(col - 1, 0), jnp.minimum(col + 1, last)
     any_peer = jnp.where(col == last, col - 1, col + 1)
     sides = ((col, after, before), (last - col, before, after))
 
-    def dequantize_down(p):
-        for i in range(pair):
-            group = p * pair + i
-            word = down_codes[pl.ds(pl.multiple_of(group * SUB, SUB), SUB), :] ^ FLIP
-            scale = down_rows[pl.ds(group, 1), :]
-            for k in range(PACK):
-                dense_down[i, k] = (nibbles(word, k) * scale).astype(jnp.bfloat16)
+    def dequantize_down(group):
+        word = down_codes[pl.ds(pl.multiple_of(group * SUB, SUB), SUB), :] ^ FLIP
+        scale = down_rows[pl.ds(group, 1), :]
+        for k in range(PACK):
+            dense_down[group, k] = (nibbles(word, k) * scale).astype(jnp.bfloat16)
 
     columns = 512 if model % 512 == 0 else GROUP
 
-    def multiply_down(p):
-        def one(i, carry):
-            lines_at = pl.ds(pl.multiple_of(i * rows_step, rows_step), rows_step)
+    def multiply_down(tau, units, hidden, target):
+        depth = target.shape[1]
+        cuts = 1
+        while (2 * depth if cuts == 1 else depth // (cuts // 2)) > 256:
+            cuts *= 2
+        for cut in range(cuts):
+            if cuts == 1:
+                at = (slice(None), slice(None))
+                height = 2 * depth
+            else:
+                height = depth * 2 // cuts
+                place = cut % (cuts // 2) * height
+                at = (pl.ds(cut // (cuts // 2), 1), pl.ds(place, height))
             left = jnp.concatenate(
-                [hidden[p * pair + c, lines_at, :] for c in range(pair)], axis=1
+                [
+                    hidden[at[0], tau * units + c, at[1], :].reshape(height, GROUP)
+                    for c in range(units)
+                ],
+                axis=1,
             )
             for n in range(0, model, columns):
-                at = pl.ds(n, columns)
-                acc[lines_at, at] += jnp.dot(
+                right = dense_down[pl.ds(tau * units, units), :, :, pl.ds(n, columns)]
+                total = jnp.dot(
                     left,
-                    dense_down[:, :, :, at].reshape(pair * GROUP, columns),
+                    right.reshape(units * GROUP, columns),
                     preferred_element_type=jnp.float32,
                 )
-            return carry
-
-        lax.fori_loop(0, total_tokens // rows_step, one, 0)
-
-    drain = last * (S_LAG + H_LAG)
+                lanes = pl.ds(n, columns)
+                old = target[at[0], at[1], lanes]
+                target[at[0], at[1], lanes] = old + total.reshape(old.shape)
+
+    def half_copy(j):
+        return remote(
+            half_send.at[j], half_got.at[j], half_ssem.at[j], half_rsem.at[j], row=sibling
+        )
+
+    def final_copy(j, target):
+        return remote(
+            comb.at[j], final_got.at[target], final_ssem.at[j], final_rsem.at[target],
+            row=other(j) + core,
+        )
+
+    def far_rows(side, j):
+        return acc_far[side, (j - 1) * count : j * count, :]
 
     def tick(t, carry):
         for i, (first, end) in enumerate(pieces):
@@ -359,67 +424,84 @@
                 @pl.when(hops == last)
                 def _():
                     value = jax.nn.silu(total[:, :GROUP]) * total[:, GROUP:]
-                    hidden[q, side_rows(side), :] = jnp.dot(
+                    value = jnp.dot(
                         value.astype(jnp.bfloat16), perm, preferred_element_type=jnp.float32
                     ).astype(jnp.bfloat16)
-                    hid_copy(side, q, backward).start()
-
-        done = t - drain
-        active = jnp.logical_and(done >= 0, lax.rem(done + pair, pair) == pair - 1)
-
-        @pl.when(done == 0)
+                    hidden_near[side, q] = value[:count]
+                    hidden_far[side, q] = value[count:]
+
+        group = t - (d_start - far_ticks)
+
+        @pl.when(group == 0)
         def _():
             down_load.wait()
             wait_down()
 
-        @pl.when(active)
-        def _():
-            dequantize_down(lax.div(done, pair))
+        @pl.when((group >= 0) & (group < chunks))
+        def _():
+            dequantize_down(group)
 
         for side, (hops, onward, backward) in enumerate(sides):
             left = last - hops
-            q = t - S_LAG * last - H_LAG * left
-
-            @pl.when((left > 0) & (q >= 0) & (q < chunks))
+            tau = t - h_start - H_LAG * left
+
+            @pl.when((tau >= 0) & (tau < far_ticks))
             def _():
-                hid_copy(side, q, any_peer).wait_recv()
+                @pl.when(left > 0)
+                def _():
+                    far_copy(side, tau, any_peer).wait_recv()
 
                 @pl.when(left < last)
                 def _():
-                    hid_copy(side, q, backward).start()
-
-        @pl.when(active)
-        def _():
-            multiply_down(lax.div(done, pair))
+                    far_copy(side, tau, backward).start()
+
+            @pl.when((tau >= far_ticks) & (tau < far_ticks + near_ticks))
+            def _():
+                @pl.when(left > 0)
+                def _():
+                    near_copy(side, tau - far_ticks, any_peer).wait_recv()
+
+                @pl.when(left < last)
+                def _():
+                    near_copy(side, tau - far_ticks, backward).start()
+
+        tau = t - d_start
+
+        @pl.when((tau >= 0) & (tau < far_ticks))
+        def _():
+            multiply_down(tau, pair, hidden_far, acc_far)
+
+        @pl.when(tau >= far_ticks)
+        def _():
+            multiply_down(tau - far_ticks, quad, hidden_near, acc_near)
+
+        @pl.when(tau == far_ticks - 1)
+        def _():
+            for j in range(chips - 1, 0, -1):
+                half_send[j] = far_rows(1 - core, j).astype(jnp.bfloat16)
+                half_copy(j).start()
+
+        @pl.when(tau == far_ticks + min(1, near_ticks - 1))
+        def _():
+            for j in range(chips - 1, 0, -1):
+                half_copy(j).wait_recv()
+                comb[j] = (far_rows(core, j) + half_got[j].astype(jnp.float32)).astype(
+                    jnp.bfloat16
+                )
+                final_copy(j, back(j)).start()
 
         return carry
 
-    lax.fori_loop(0, chunks + drain, tick, 0)
-
-    def half_copy(j):
-        return remote(
-            half_send.at[j], half_got.at[j], half_ssem.at[j], half_rsem.at[j], row=sibling
-        )
-
-    def final_copy(j, target):
-        return remote(
-            comb.at[j], final_got.at[target], final_ssem.at[j], final_rsem.at[target],
-            row=other(j) + core,
-        )
-
-    for j in range(chips - 1, -1, -1):
-        half_send[j] = acc[block(1 - core, j), :].astype(jnp.bfloat16)
-        half_copy(j).start()
-    for j in range(chips - 1, 0, -1):
-        half_copy(j).wait_recv()
-        comb[j] = (acc[block(core, j), :] + half_got[j].astype(jnp.float32)).astype(jnp.bfloat16)
-        final_copy(j, back(j)).start()
-    half_copy(0).wait_recv()
-    total = acc[block(core, 0), :] + half_got[0].astype(jnp.float32)
+    lax.fori_loop(0, d_start + far_ticks + near_ticks, tick, 0)
+
+    half_send[0] = acc_near[1 - core].astype(jnp.bfloat16)
+    half_copy(0).start()
+    total = acc_near[core]
     for j in range(1, chips):
         final_copy(back(j), j).wait_recv()
         total = total + final_got[j].astype(jnp.float32)
-    out[...] = total.astype(jnp.bfloat16)
+    half_copy(0).wait_recv()
+    out[...] = (total + half_got[0].astype(jnp.float32)).astype(jnp.bfloat16)
 
     for j in range(1, chips):
         token_copy(j, back(j)).wait_send()
@@ -436,19 +518,28 @@
                     scale_copy(kind, i, step).wait_send()
             down_copy(step).wait_send()
 
-    def sent(q, carry):
+    def sent_sums(q, carry):
         for side, (hops, onward, backward) in enumerate(sides):
             @pl.when(hops < last)
             def _():
                 sum_copy(side, q, got.at[side, q], any_peer).wait_send()
 
-            @pl.when(hops > 0)
-            def _():
-                hid_copy(side, q, any_peer).wait_send()
-
         return carry
 
-    lax.fori_loop(0, chunks, sent, 0)
+    def sent_hidden(copy_of):
+        def one(tau, carry):
+            for side, (hops, onward, backward) in enumerate(sides):
+                @pl.when(hops > 0)
+                def _():
+                    copy_of(side, tau, any_peer).wait_send()
+
+            return carry
+
+        return one
+
+    lax.fori_loop(0, chunks, sent_sums, 0)
+    lax.fori_loop(0, far_ticks, sent_hidden(far_copy), 0)
+    lax.fori_loop(0, near_ticks, sent_hidden(near_copy), 0)
 
 
 def layer(tokens, gate, up, down, gate_scale, up_scale, down_scale, rows, cols):
@@ -458,13 +549,14 @@
     share = rows // cols
     down_groups = down_scale.shape[1] // rows
     span = down_scale.shape[0]
-    down_scale = down_scale.T.reshape(rows, down_groups, span)
+    lines_down = -(-down_groups // 16) * 16
     chunks = width // GROUP
     chips = rows // 2
     tokens_all = count * rows
     half = tokens_all // 2
     groups = share * lines
-    pair = 2 if chunks % 2 == 0 else 1
+    pair, quad = 2 - chunks % 2, 4 if chunks % 4 == 0 else 1
+    steps = chunks // pair + chunks // quad
     parts = len(pieces_of(chunks))
     any_spec = pl.BlockSpec(memory_space=pl.ANY)
     bf16, f32, i32 = jnp.bfloat16, jnp.float32, jnp.int32
@@ -479,22 +571,28 @@
             pltpu.VMEM((words, width), i32),
             pltpu.VMEM((words, width), i32),
             pltpu.VMEM(down.shape, i32),
+            pltpu.VMEM(gate_scale.shape, bf16),
+            pltpu.VMEM(up_scale.shape, bf16),
+            pltpu.VMEM(down_scale.shape, bf16),
+            pltpu.VMEM((rows, lines_down, span), bf16),
             pltpu.VMEM((share, lines, width), bf16),
             pltpu.VMEM((share, lines, width), bf16),
-            pltpu.VMEM((share, down_groups, span), bf16),
+            pltpu.VMEM((share, lines_down, span), bf16),
             pltpu.VMEM((2, groups, GROUP), f32),
-            pltpu.VMEM((down_groups, share * span), f32),
+            pltpu.VMEM((lines_down, share * span), f32),
             pltpu.VMEM((groups, PACK, SUB, 2 * GROUP), bf16),
-            pltpu.VMEM((pair, PACK, SUB, model), bf16),
+            pltpu.VMEM((chunks, PACK, SUB, model), bf16),
             pltpu.VMEM((chunks, tokens_all, 2 * GROUP), bf16),
             pltpu.VMEM((2, chunks, half, 2 * GROUP), bf16),
-            pltpu.VMEM((chunks, tokens_all, GROUP), bf16),
-            pltpu.VMEM((tokens_all, model), f32),
+            pltpu.VMEM((2, chunks, half - count, GROUP), bf16),
+            pltpu.VMEM((2, chunks, count, GROUP), bf16),
+            pltpu.VMEM((2, half - count, model), f32),
+            pltpu.VMEM((2, count, model), f32),
             pltpu.VMEM((chips, count, model), bf16),
             pltpu.VMEM((chips, count, model), bf16),
             pltpu.VMEM((chips, count, model), bf16),
             pltpu.VMEM((chips, count, model), bf16),
-            DMA((2 + 2 * parts,)),
+            DMA((5 + 2 * parts,)),
             DMA((chips,)),
             DMA((chips,)),
             DMA((chips,)),
@@ -505,8 +603,8 @@
             DMA((share,)),
             DMA((2, chunks)),
             DMA((2, chunks)),
-            DMA((2, chunks)),
-            DMA((2, chunks)),
+            DMA((2, steps)),
+            DMA((2, steps)),
             DMA((chips,)),
             DMA((chips,)),
             DMA((chips,)),

time: 106 us -> 98.1 us (0.925)
  Pallas kernels: 102 us -> 94.3 us
    pallas_call x1, Pallas kernels: 102 us -> 94.3 us  [layer(): pl.pallas_call(functools.partial(layer_kernel, rows, cols, chunks), in_sp...]
    unnamed x1 -> x2, local copies, waits for them, and re-layouts: 1.57 us -> 3.58 us
    reshape x1 -> x0, local copies, waits for them, and re-layouts: 1.9 us -> none  [layer(): down_scale = down_scale.T.reshape(rows, down_groups, span)]
where the time goes in v2:
time: 98.1 us; the launch traced here: 97.9 us
  Pallas kernels  94.3 us (96%)
  local copies, waits for them, and re-layouts  3.58 us (4%)
    pallas_call x1, Pallas kernels, layer(): pl.pallas_call(functools.partial(layer_kernel, rows, cols, chunks), in_sp...  94.3 us
    unnamed x2, local copies, waits for them, and re-layouts  3.58 us

profile of v2, /device:TPU:0, one launch (start us, length us, event | category | flops | bytes accessed | tf_op | source)
XLA Modules:
  0.0 97.9 jit_solution(6070668744293404269)
XLA Ops:
  0.0 2.0 %copy.8.down_scale = bf16[1024,224]{1,0:T(8,128)(2,1)} copy(bf16[1024,224]{0,1:T(8,128)(2,1)} %param.13) | data formatting | bytes 917504 | tf_op args[6]
  2.0 94.3 %layer.1 = bf16[32,2048]{1,0:T(8,128)(2,1)} custom-call(bf16[32,2048]{1,0:T(8,128)(2,1)} %tokens.1, s32[256,3584]{1,0:T(8,128)} %gate.1, s32[256,3584]{1,0:T(8,128)} %up.1, s32[448,2048]{1,0:T(8,128)} %down.1, bf16[8,28672]{1,0:T(8,128)(2,1)} %gate_scale.1, bf16[8,28672]{1,0:T(8,128)(2,1)} %up_scale.1, bf16[1024,224]{1,0:T(8,128)(2,1)} %copy.8.down_scale), custom_call_target="tpu_custom_call" | custom-call | tf_op jit(solution)/shard_map/layer/pallas_call | solution.py:563
  96.3 1.6 %copy.10 = bf16[32,2048]{1,0:T(8,128)(2,1)} copy(bf16[32,2048]{1,0:T(8,128)(2,1)} %layer.1) | data formatting | bytes 262144

commit v3 on v2

v3 whole, which is shorter than its diff:
```python
import functools

import jax
import jax.numpy as jnp
from jax import lax
from jax.experimental import pallas as pl
from jax.experimental.pallas import tpu as pltpu
from jax.sharding import PartitionSpec as P

GROUP = 128
PACK = 8
SUB = GROUP // PACK
MESH = pl.DeviceIdType.MESH
DMA = pltpu.SemaphoreType.DMA
S_LAG = 3
H_LAG = 5
H_WAIT = 0
PARTS = 1
EARLY = 2
FLIP = -2004318072


def permutation():
    source = lax.broadcasted_iota(jnp.int32, (GROUP, GROUP), 0)
    target = lax.broadcasted_iota(jnp.int32, (GROUP, GROUP), 1)
    wanted = lax.rem(target, SUB) * PACK + lax.div(target, SUB)
    return (source == wanted).astype(jnp.bfloat16)


def pieces_of(chunks):
    bounds = sorted({0, 1, max(1, chunks // 7), max(1, 3 * chunks // 7), chunks})
    return list(zip(bounds[:-1], bounds[1:]))


def nibbles(word, k):
    code = word if k == PACK - 1 else jnp.left_shift(word, 28 - 4 * k)
    return jnp.right_shift(code, 28).astype(jnp.float32)


def layer_kernel(
    rows, cols, chunks,
    tokens, gate, up, down, gate_scale, up_scale, down_scale, out,
    all_tokens, moved, gate_codes, up_codes, down_codes,
    gate_own, up_own, down_own, down_turned,
    gate_got, up_got, down_got, unit_scale, down_rows,
    dense, dense_down, sums, got,
    hidden, acc,
    half_send, half_got, comb, final_got,
    local_sem, token_send, token_recv, relay_send, relay_recv,
    scale_send, scale_recv, down_recv,
    sum_send, sum_recv, hid_send, hid_recv,
    half_ssem, half_rsem, final_ssem, final_rsem,
):
    row, col = lax.axis_index("row"), lax.axis_index("col")
    core = lax.rem(row, 2)
    chip = row - core
    sibling = row + 1 - 2 * core
    chips = rows // 2
    share = rows // cols
    last = cols - 1
    count, model = tokens.shape
    total_tokens = count * rows
    half = total_tokens // 2
    width = gate.shape[1]
    lines = gate_scale.shape[0]
    groups = share * lines
    part = half // PARTS
    pair, quad = 2 - chunks % 2, 4 if chunks % 4 == 0 else 1
    pieces = pieces_of(chunks)
    home = lax.div(row, share) == col
    slot = lax.rem(row, share)
    exact = chips & (chips - 1) == 0

    def other(j):
        if not exact:
            return lax.rem(chip + 2 * j, rows)
        peer, bit = chip, 2
        while bit <= 2 * j:
            if (2 * j) & bit:
                peer = peer + bit - 2 * bit * lax.rem(lax.div(chip, bit), 2)
            bit *= 2
        return peer

    def back(j):
        return j if exact else (chips - j) % chips

    def block(side, j):
        return pl.ds(pl.multiple_of((side * chips + j) * count, count), count)

    def remote(source, target, send, recv, **where):
        return pltpu.make_async_remote_copy(
            src_ref=source, dst_ref=target, send_sem=send, recv_sem=recv,
            device_id=where, device_id_type=MESH,
        )

    own_copy = pltpu.make_async_copy(tokens, all_tokens.at[block(core, 0)], local_sem.at[0])
    own_copy.start()

    def code_copies(i):
        first, end = pieces[i]
        at = pl.ds(first * GROUP, (end - first) * GROUP)
        return [
            pltpu.make_async_copy(gate.at[:, at], gate_codes.at[:, at], local_sem.at[2 + 2 * i]),
            pltpu.make_async_copy(up.at[:, at], up_codes.at[:, at], local_sem.at[3 + 2 * i]),
        ]

    for copy in code_copies(0):
        copy.start()
    first_code = 2 + 2 * len(pieces)
    scale_loads = [
        pltpu.make_async_copy(source, target, local_sem.at[first_code + i])
        for i, (source, target) in enumerate(
            ((gate_scale, gate_own), (up_scale, up_own), (down_scale, down_own))
        )
    ]

    @pl.when(home)
    def _():
        for load in scale_loads:
            load.start()

    barrier = pltpu.get_barrier_semaphore()
    for step in range(1, rows):
        pl.semaphore_signal(
            barrier, inc=1, device_id={"row": lax.rem(row + step, rows)}, device_id_type=MESH
        )

    @pl.when(col > 0)
    def _():
        pl.semaphore_signal(barrier, inc=1, device_id={"col": col - 1}, device_id_type=MESH)

    @pl.when(col < last)
    def _():
        pl.semaphore_signal(barrier, inc=1, device_id={"col": col + 1}, device_id_type=MESH)

    inner = jnp.logical_and(col > 0, col < last)

    @pl.when(inner)
    def _():
        pl.semaphore_wait(barrier, rows + 1)

    @pl.when(jnp.logical_not(inner))
    def _():
        pl.semaphore_wait(barrier, rows)

    def scale_copy(kind, i, step):
        first, end = pieces[i]
        peer = lax.rem(row + step, rows)
        span = (end - first) * GROUP
        source, target = ((gate_own, gate_got), (up_own, up_got))[kind]
        source = source.at[:, pl.ds(pl.multiple_of(peer * width + first * GROUP, GROUP), span)]
        target = target.at[slot, :, pl.ds(first * GROUP, span)]
        if step == 0:
            return pltpu.make_async_copy(source, target, scale_recv.at[kind, i, slot])
        return remote(
            source, target, scale_send.at[kind], scale_recv.at[kind, i, slot], row=peer
        )

    def down_copy(step):
        peer = lax.rem(row + step, rows)
        if step == 0:
            return pltpu.make_async_copy(
                down_turned.at[peer], down_got.at[slot], down_recv.at[slot]
            )
        return remote(
            down_turned.at[peer], down_got.at[slot], scale_send.at[2], down_recv.at[slot], row=peer
        )

    def start_scales(i):
        @pl.when(home)
        def _():
            for step in range(rows):
                for kind in range(2):
                    scale_copy(kind, i, step).start()

    def wait_slot(copy_of, t, finish):
        here = row == col * share + t

        @pl.when(here)
        def _():
            copy_of(0).wait()

        @pl.when(jnp.logical_not(here))
        def _():
            finish().wait_recv()

    def wait_scales(i):
        first, end = pieces[i]
        at = pl.ds(first * GROUP, (end - first) * GROUP)
        peer = lax.rem(row + 1, rows)
        for t in range(share):
            for kind, target in enumerate((gate_got, up_got)):
                source = (gate_own, up_own)[kind]
                wait_slot(
                    lambda step: scale_copy(kind, i, step),
                    t,
                    lambda: remote(
                        source.at[:, at], target.at[t, :, at], scale_send.at[kind],
                        scale_recv.at[kind, i, t], row=peer,
                    ),
                )

    def wait_down():
        peer = lax.rem(row + 1, rows)
        span = down_got.shape[2]
        for t in range(share):
            wait_slot(
                down_copy,
                t,
                lambda: remote(
                    down_turned.at[0], down_got.at[t], scale_send.at[2], down_recv.at[t], row=peer
                ),
            )
        for t in range(share):
            down_rows[:, t * span : (t + 1) * span] = down_got[t].astype(jnp.float32)

    crossed = exact and chips == 4 and count % 32 == 0
    piece = count // 2

    def token_copy(source, target, peer, slice_index=None):
        def at(j):
            if slice_index is None:
                return block(core, j)
            first = (core * chips + j) * count + slice_index * piece
            return pl.ds(pl.multiple_of(first, piece), piece)

        index = 2 * target + (slice_index or 0)
        return remote(
            all_tokens.at[at(source)], all_tokens.at[at(target)],
            token_send.at[index], token_recv.at[index], row=other(peer) + core,
        )

    def relay(j):
        return remote(
            all_tokens.at[block(core, j)], all_tokens.at[block(core, j)],
            relay_send.at[j], relay_recv.at[j], row=sibling,
        )

    if crossed:
        token_sends = [token_copy(0, j, j, p) for j, p in ((1, 0), (2, 1), (1, 1), (2, 0))]
        token_hands = [token_copy(1, 3, 2, 0), token_copy(2, 3, 1, 1)]
    else:
        token_sends = [token_copy(0, back(j), j) for j in range(chips - 1, 0, -1)]
        token_hands = []

    @pl.when(home)
    def _():
        for load in scale_loads:
            load.wait()

    start_scales(0)
    own_copy.wait()
    def send_scales():
        for i in range(1, len(pieces)):
            start_scales(i)
            for copy in code_copies(i):
                copy.start()

        @pl.when(home)
        def _():
            down_groups = down_own.shape[1] // rows
            line = lax.broadcasted_iota(jnp.int32, (rows * down_got.shape[1], down_own.shape[1]), 0)
            wanted = lax.broadcasted_iota(jnp.int32, line.shape, 1)
            owner = lax.div(line, down_got.shape[1])
            group = lax.rem(line, down_got.shape[1])
            pick = (wanted == owner * down_groups + group) & (group < down_groups)
            turned = lax.dot_general(
                pick.astype(jnp.bfloat16), down_own[...], (((1,), (1,)), ((), ())),
                preferred_element_type=jnp.float32,
            )
            down_turned[...] = turned.astype(jnp.bfloat16).reshape(down_turned.shape)
            for step in range(rows):
                down_copy(step).start()

    for copy in token_sends:
        copy.start()
    relay(0).start()
    down_load = pltpu.make_async_copy(down, down_codes, local_sem.at[1])
    down_load.start()
    acc[...] = jnp.zeros_like(acc)
    batch = 4 if groups % 4 == 0 else 1

    def dequantize_up(t):
        at = pl.ds(pl.multiple_of(t * GROUP, GROUP), GROUP)
        for kind, (codes, scale) in enumerate(((gate_codes, gate_got), (up_codes, up_got))):
            for s in range(share):
                unit_scale[kind, s * lines : (s + 1) * lines, :] = scale[s, :, at].astype(jnp.float32)

        def one(b, carry):
            for kind, codes in enumerate((gate_codes, up_codes)):
                word = codes[pl.ds(pl.multiple_of(b * batch * SUB, SUB), batch * SUB), at] ^ FLIP
                word = word.reshape(batch, SUB, GROUP)
                scale = jnp.stack(
                    [unit_scale[kind, pl.ds(b * batch + i, 1), :] for i in range(batch)]
                )
                for k in range(PACK):
                    value = (nibbles(word, k) * scale).astype(jnp.bfloat16)
                    dense[pl.ds(b * batch, batch), k, :, kind * GROUP : (kind + 1) * GROUP] = value
            return carry

        lax.fori_loop(0, groups // batch, one, 0)

    def ready(i):
        for copy in code_copies(i):
            copy.wait()
        wait_scales(i)

    if crossed:
        for copy, hand in zip(token_sends[:2], token_hands):
            copy.wait_recv()
            hand.start()
        send_scales()
        for j, copy in zip((1, 2), token_sends[2:]):
            copy.wait_recv()
            relay(j).start()
        ready(0)
        dequantize_up(0)
        for hand in token_hands:
            hand.wait_recv()
        relay(3).start()
    else:
        send_scales()
        for j in range(1, chips):
            token_copy(0, j, back(j)).wait_recv()
            relay(j).start()
        ready(0)
        dequantize_up(0)
    for j in range(chips):
        relay(j).wait_recv()

    rows_step = min(total_tokens, 256)
    perm = permutation()

    def permute(i, carry):
        lines_at = pl.ds(pl.multiple_of(i * rows_step, rows_step), rows_step)
        for group in range(model // GROUP):
            at = pl.ds(group * GROUP, GROUP)
            moved[lines_at, at] = jnp.dot(
                all_tokens[lines_at, at], perm, preferred_element_type=jnp.float32
            ).astype(jnp.bfloat16)
        return carry

    lax.fori_loop(0, total_tokens // rows_step, permute, 0)

    def multiply_up(t):
        def multiply(i, carry):
            lines_at = pl.ds(pl.multiple_of(i * rows_step, rows_step), rows_step)
            total = jnp.dot(
                moved[lines_at, :],
                dense[...].reshape(model, 2 * GROUP),
                preferred_element_type=jnp.float32,
            )
            sums[t, lines_at, :] = total.astype(jnp.bfloat16)
            return carry

        lax.fori_loop(0, total_tokens // rows_step, multiply, 0)

    def side_rows(side):
        return pl.ds(side * half, half)

    def sum_copy(side, q, p, source, peer):
        at = pl.ds(p * part, part)
        index = q * PARTS + p
        return remote(
            source, got.at[side, q, at], sum_send.at[side], sum_recv.at[side, index], col=peer
        )

    per_chip = chunks // quad
    steps = chips * per_chip

    early = min(EARLY, per_chip - 1)
    late = per_chip - early

    def piece_of(tau):
        rest = tau - chips * early
        soon = rest < 0
        j = jnp.where(soon, lax.rem(tau, chips), lax.div(jnp.maximum(rest, 0), late))
        k = jnp.where(
            soon, lax.div(tau, chips), early + lax.rem(jnp.maximum(rest, 0), late)
        )
        return chips - 1 - j, k * quad

    def hid_copy(side, tau, peer):
        j, first = piece_of(tau)
        ref = hidden.at[side, j, pl.ds(first, quad)]
        return remote(ref, ref, hid_send.at[side], hid_recv.at[side, tau], col=peer)

    h_start = last * S_LAG + H_WAIT + max(quad - 1, chunks - chips * early - late)
    d_start = h_start + last * H_LAG

    before, after = jnp.maximum(col - 1, 0), jnp.minimum(col + 1, last)
    any_peer = jnp.where(col == last, col - 1, col + 1)
    sides = ((col, after, before), (last - col, before, after))

    def dequantize_down(group):
        word = down_codes[pl.ds(pl.multiple_of(group * SUB, SUB), SUB), :] ^ FLIP
        scale = down_rows[pl.ds(group, 1), :]
        for k in range(PACK):
            dense_down[group, k] = (nibbles(word, k) * scale).astype(jnp.bfloat16)

    columns = 512 if model % 512 == 0 else GROUP

    def multiply_down(tau):
        j, first = piece_of(tau)
        left = jnp.concatenate(
            [hidden[:, j, first + c].reshape(2 * count, GROUP) for c in range(quad)], axis=1
        )
        for n in range(0, model, columns):
            at = pl.ds(n, columns)
            right = dense_down[pl.ds(first, quad), :, :, at].reshape(quad * GROUP, columns)
            total = jnp.dot(left, right, preferred_element_type=jnp.float32)
            acc[j, :, :, at] += total.reshape(2, count, columns)

    def half_copy(j):
        return remote(
            half_send.at[j], half_got.at[j], half_ssem.at[j], half_rsem.at[j], row=sibling
        )

    def final_copy(j, target):
        return remote(
            comb.at[j], final_got.at[target], final_ssem.at[j], final_rsem.at[target],
            row=other(j) + core,
        )

    def give_sibling(j):
        half_send[j] = acc[j, 1 - core].astype(jnp.bfloat16)
        half_copy(j).start()

    def give_chip(j):
        half_copy(j).wait_recv()
        comb[j] = (acc[j, core] + half_got[j].astype(jnp.float32)).astype(jnp.bfloat16)
        final_copy(j, back(j)).start()

    def sent_early():
        for copy in token_sends + token_hands:
            copy.wait_send()
        for j in range(chips):
            relay(j).wait_send()

        @pl.when(home)
        def _():
            most = pl.ds(0, (rows - 1) * width)
            for kind, ref in enumerate((gate_own.at[:, most], up_own.at[:, most])):
                remote(
                    ref, ref, scale_send.at[kind], scale_recv.at[kind, 0, 0], row=sibling
                ).wait_send()
            ref = down_turned.at[pl.ds(0, rows - 1)]
            remote(ref, ref, scale_send.at[2], down_recv.at[0], row=sibling).wait_send()

    def tick(t, carry):
        @pl.when(t < chunks)
        def _():
            multiply_up(t)
            for side, (hops, onward, backward) in enumerate(sides):
                @pl.when(hops == 0)
                def _():
                    for p in range(PARTS):
                        own = sums.at[t, pl.ds(side * half + p * part, part)]
                        sum_copy(side, t, p, own, onward).start()

        for i, (first, end) in enumerate(pieces[1:], 1):
            @pl.when(t + 1 == first)
            def _():
                ready(i)

        @pl.when(t + 1 < chunks)
        def _():
            dequantize_up(t + 1)

        for side, (hops, onward, backward) in enumerate(sides):
            q = t - S_LAG * hops

            @pl.when((hops > 0) & (q >= 0) & (q < chunks))
            def _():
                @pl.when(hops < last)
                def _():
                    for p in range(PARTS):
                        at = pl.ds(p * part, part)
                        own = sums[q, pl.ds(side * half + p * part, part), :]
                        sum_copy(side, q, p, got.at[side, q, at], any_peer).wait_recv()
                        total = got[side, q, at, :].astype(jnp.float32) + own.astype(jnp.float32)
                        got[side, q, at, :] = total.astype(jnp.bfloat16)
                        sum_copy(side, q, p, got.at[side, q, at], onward).start()

                @pl.when(hops == last)
                def _():
                    for p in range(PARTS):
                        at = pl.ds(p * part, part)
                        sum_copy(side, q, p, got.at[side, q, at], any_peer).wait_recv()
                    total = got[side, q].astype(jnp.float32) + sums[
                        q, side_rows(side), :
                    ].astype(jnp.float32)
                    value = jax.nn.silu(total[:, :GROUP]) * total[:, GROUP:]
                    value = jnp.dot(
                        value.astype(jnp.bfloat16), perm, preferred_element_type=jnp.float32
                    ).astype(jnp.bfloat16)
                    for j in range(chips):
                        hidden[side, j, q] = value[j * count : (j + 1) * count]

        group = (t - chunks) * pair

        @pl.when(group == 0)
        def _():
            down_load.wait()
            wait_down()

        @pl.when((group >= 0) & (group < chunks))
        def _():
            for i in range(pair):
                dequantize_down(group + i)

        for side, (hops, onward, backward) in enumerate(sides):
            left = last - hops
            tau = t - h_start - H_LAG * left

            @pl.when((tau >= 0) & (tau < steps))
            def _():
                @pl.when(left > 0)
                def _():
                    hid_copy(side, tau, any_peer).wait_recv()

                @pl.when(left < last)
                def _():
                    hid_copy(side, tau, backward).start()

        tau = t - d_start

        @pl.when(tau >= 0)
        def _():
            multiply_down(tau)

        for j in range(chips - 1, 0, -1):
            done = chips * early + (chips - j) * late

            @pl.when(tau == done - 1)
            def _():
                give_sibling(j)

            @pl.when(tau == done + min(1, late - 1))
            def _():
                give_chip(j)

        @pl.when(t == chunks)
        def _():
            sent_early()

        return carry

    lax.fori_loop(0, d_start + steps, tick, 0)

    half_send[0] = acc[0, 1 - core].astype(jnp.bfloat16)
    half_copy(0).start()
    total = acc[0, core]
    for j in range(1, chips):
        final_copy(back(j), j).wait_recv()
        total = total + final_got[j].astype(jnp.float32)
    half_copy(0).wait_recv()
    out[...] = (total + half_got[0].astype(jnp.float32)).astype(jnp.bfloat16)

    for j in range(1, chips):
        final_copy(j, back(j)).wait_send()
    for j in range(chips):
        half_copy(j).wait_send()
    for side, (hops, onward, backward) in enumerate(sides):
        @pl.when(hops < last)
        def _():
            ref = got.at[side]
            remote(ref, ref, sum_send.at[side], sum_recv.at[side, 0], col=any_peer).wait_send()

        @pl.when(hops > 0)
        def _():
            ref = hidden.at[side]
            remote(ref, ref, hid_send.at[side], hid_recv.at[side, 0], col=any_peer).wait_send()


def layer(tokens, gate, up, down, gate_scale, up_scale, down_scale, rows, cols):
    count, model = tokens.shape
    words, width = gate.shape
    lines = gate_scale.shape[0]
    share = rows // cols
    down_groups = down_scale.shape[1] // rows
    span = down_scale.shape[0]
    lines_down = -(-down_groups // 16) * 16
    chunks = width // GROUP
    chips = rows // 2
    tokens_all = count * rows
    half = tokens_all // 2
    groups = share * lines
    pair, quad = 2 - chunks % 2, 4 if chunks % 4 == 0 else 1
    steps = chips * (chunks // quad)
    parts = len(pieces_of(chunks))
    any_spec = pl.BlockSpec(memory_space=pl.ANY)
    bf16, f32, i32 = jnp.bfloat16, jnp.float32, jnp.int32
    return pl.pallas_call(
        functools.partial(layer_kernel, rows, cols, chunks),
        in_specs=[any_spec] * 7,
        out_specs=pl.BlockSpec(memory_space=pltpu.VMEM),
        out_shape=jax.ShapeDtypeStruct((count, model), bf16),
        scratch_shapes=[
            pltpu.VMEM((tokens_all, model), bf16),
            pltpu.VMEM((tokens_all, model), bf16),
            pltpu.VMEM((words, width), i32),
            pltpu.VMEM((words, width), i32),
            pltpu.VMEM(down.shape, i32),
            pltpu.VMEM(gate_scale.shape, bf16),
            pltpu.VMEM(up_scale.shape, bf16),
            pltpu.VMEM(down_scale.shape, bf16),
            pltpu.VMEM((rows, lines_down, span), bf16),
            pltpu.VMEM((share, lines, width), bf16),
            pltpu.VMEM((share, lines, width), bf16),
            pltpu.VMEM((share, lines_down, span), bf16),
            pltpu.VMEM((2, groups, GROUP), f32),
            pltpu.VMEM((lines_down, share * span), f32),
            pltpu.VMEM((groups, PACK, SUB, 2 * GROUP), bf16),
            pltpu.VMEM((chunks, PACK, SUB, model), bf16),
            pltpu.VMEM((chunks, tokens_all, 2 * GROUP), bf16),
            pltpu.VMEM((2, chunks, half, 2 * GROUP), bf16),
            pltpu.VMEM((2, chips, chunks, count, GROUP), bf16),
            pltpu.VMEM((chips, 2, count, model), f32),
            pltpu.VMEM((chips, count, model), bf16),
            pltpu.VMEM((chips, count, model), bf16),
            pltpu.VMEM((chips, count, model), bf16),
            pltpu.VMEM((chips, count, model), bf16),
            DMA((5 + 2 * parts,)),
            DMA((2 * chips,)),
            DMA((2 * chips,)),
            DMA((chips,)),
            DMA((chips,)),
            DMA((3,)),
            DMA((2, parts, share)),
            DMA((share,)),
            DMA((2,)),
            DMA((2, chunks * PARTS)),
            DMA((2,)),
            DMA((2, steps)),
            DMA((chips,)),
            DMA((chips,)),
            DMA((chips,)),
            DMA((chips,)),
        ],
        compiler_params=pltpu.CompilerParams(
            collective_id=0, has_side_effects=True, vmem_limit_bytes=60 * 1024 * 1024
        ),
        name="layer",
    )(tokens, gate, up, down, gate_scale, up_scale, down_scale)


def per_device(tokens, gate_codes, up_codes, down_codes, gate_scales, up_scales, down_scales):
    rows, cols = lax.axis_size("row"), lax.axis_size("col")
    return layer(
        tokens, gate_codes, up_codes, down_codes, gate_scales, up_scales, down_scales, rows, cols
    )


def solution(mesh):
    placed = (
        P("row", "col"),
        P("col", "row"),
        P("col", "row"),
        P("row", "col"),
        P("row", None),
        P("row", None),
        P("row", None),
    )
    return jax.shard_map(
        per_device, mesh=mesh, in_specs=placed, out_specs=P("row", "col"), check_vma=False
    )
```

time: 98.1 us -> 95.2 us (0.970)
  Pallas kernels: 94.3 us -> 91.5 us
    pallas_call x1, Pallas kernels: 94.3 us -> 91.5 us  [layer(): pl.pallas_call(functools.partial(layer_kernel, rows, cols, chunks), in_sp...]
where the time goes in v3:
time: 95.2 us; the launch traced here: 95.1 us
  Pallas kernels  91.5 us (96%)
  local copies, waits for them, and re-layouts  3.58 us (4%)
    pallas_call x1, Pallas kernels, layer(): pl.pallas_call(functools.partial(layer_kernel, rows, cols, chunks), in_sp...  91.5 us
    unnamed x2, local copies, waits for them, and re-layouts  3.58 us

profile of v3, /device:TPU:0, one launch (start us, length us, event | category | flops | bytes accessed | tf_op | source)
XLA Modules:
  0.0 95.1 jit_solution(7362155035673224370)
XLA Ops:
  0.0 2.0 %copy.8.down_scale = bf16[1024,224]{1,0:T(8,128)(2,1)} copy(bf16[1024,224]{0,1:T(8,128)(2,1)} %param.13) | data formatting | bytes 917504 | tf_op args[6]
  2.0 91.5 %layer.1 = bf16[32,2048]{1,0:T(8,128)(2,1)} custom-call(bf16[32,2048]{1,0:T(8,128)(2,1)} %tokens.1, s32[256,3584]{1,0:T(8,128)} %gate.1, s32[256,3584]{1,0:T(8,128)} %up.1, s32[448,2048]{1,0:T(8,128)} %down.1, bf16[8,28672]{1,0:T(8,128)(2,1)} %gate_scale.1, bf16[8,28672]{1,0:T(8,128)(2,1)} %up_scale.1, bf16[1024,224]{1,0:T(8,128)(2,1)} %copy.8.down_scale), custom_call_target="tpu_custom_call" | custom-call | tf_op jit(solution)/shard_map/layer/pallas_call | solution.py:594
  93.5 1.6 %copy.10 = bf16[32,2048]{1,0:T(8,128)(2,1)} copy(bf16[32,2048]{1,0:T(8,128)(2,1)} %layer.1) | data formatting | bytes 262144

commit v4 on v3

--- a/solution.py
+++ b/solution.py
@@ -16,7 +16,7 @@
 H_LAG = 5
 H_WAIT = 0
 PARTS = 1
-EARLY = 2
+EARLY = 1
 FLIP = -2004318072
 
 
@@ -214,19 +214,21 @@
         for t in range(share):
             down_rows[:, t * span : (t + 1) * span] = down_got[t].astype(jnp.float32)
 
-    crossed = exact and chips == 4 and count % 32 == 0
+    crossed = exact and chips == 4 and count % 32 == 0 and model % (2 * GROUP) == 0
     piece = count // 2
 
-    def token_copy(source, target, peer, slice_index=None):
+    def token_copy(source, target, peer, slice_index=None, lane=0):
+        lanes = slice(None) if slice_index is None else pl.ds(lane * (model // 2), model // 2)
+
         def at(j):
             if slice_index is None:
                 return block(core, j)
             first = (core * chips + j) * count + slice_index * piece
             return pl.ds(pl.multiple_of(first, piece), piece)
 
-        index = 2 * target + (slice_index or 0)
+        index = 4 * target + 2 * (slice_index or 0) + lane
         return remote(
-            all_tokens.at[at(source)], all_tokens.at[at(target)],
+            all_tokens.at[at(source), lanes], all_tokens.at[at(target), lanes],
             token_send.at[index], token_recv.at[index], row=other(peer) + core,
         )
 
@@ -237,8 +239,15 @@
         )
 
     if crossed:
-        token_sends = [token_copy(0, j, j, p) for j, p in ((1, 0), (2, 1), (1, 1), (2, 0))]
-        token_hands = [token_copy(1, 3, 2, 0), token_copy(2, 3, 1, 1)]
+        token_sends = [
+            token_copy(0, j, j, p, lane)
+            for order in (((1, 0), (2, 1)), ((1, 1), (2, 0)))
+            for lane in range(2)
+            for j, p in order
+        ]
+        token_hands = [
+            token_copy(j, 3, 3 - j, j - 1, lane) for lane in range(2) for j in (1, 2)
+        ]
     else:
         token_sends = [token_copy(0, back(j), j) for j in range(chips - 1, 0, -1)]
         token_hands = []
@@ -250,8 +259,13 @@
 
     start_scales(0)
     own_copy.wait()
+    def send_soon():
+        start_scales(1)
+        for copy in code_copies(1):
+            copy.start()
+
     def send_scales():
-        for i in range(1, len(pieces)):
+        for i in range(2, len(pieces)):
             start_scales(i)
             for copy in code_copies(i):
                 copy.start()
@@ -306,19 +320,22 @@
         wait_scales(i)
 
     if crossed:
-        for copy, hand in zip(token_sends[:2], token_hands):
+        for copy, hand in zip(token_sends[:4], token_hands):
             copy.wait_recv()
             hand.start()
-        send_scales()
-        for j, copy in zip((1, 2), token_sends[2:]):
+        send_soon()
+        for copy in token_sends[4:]:
             copy.wait_recv()
-            relay(j).start()
+        relay(1).start()
+        relay(2).start()
         ready(0)
         dequantize_up(0)
         for hand in token_hands:
             hand.wait_recv()
         relay(3).start()
+        send_scales()
     else:
+        send_soon()
         send_scales()
         for j in range(1, chips):
             token_copy(0, j, back(j)).wait_recv()
@@ -400,16 +417,19 @@
 
     columns = 512 if model % 512 == 0 else GROUP
 
-    def multiply_down(tau):
-        j, first = piece_of(tau)
+    def multiply_down(first, j, size):
         left = jnp.concatenate(
-            [hidden[:, j, first + c].reshape(2 * count, GROUP) for c in range(quad)], axis=1
+            [
+                hidden[:, pl.ds(j, size), first + c].reshape(2 * size * count, GROUP)
+                for c in range(quad)
+            ],
+            axis=1,
         )
         for n in range(0, model, columns):
             at = pl.ds(n, columns)
             right = dense_down[pl.ds(first, quad), :, :, at].reshape(quad * GROUP, columns)
             total = jnp.dot(left, right, preferred_element_type=jnp.float32)
-            acc[j, :, :, at] += total.reshape(2, count, columns)
+            acc[:, pl.ds(j, size), :, at] += total.reshape(2, size, count, columns)
 
     def half_copy(j):
         return remote(
@@ -423,12 +443,12 @@
         )
 
     def give_sibling(j):
-        half_send[j] = acc[j, 1 - core].astype(jnp.bfloat16)
+        half_send[j] = acc[1 - core, j].astype(jnp.bfloat16)
         half_copy(j).start()
 
     def give_chip(j):
         half_copy(j).wait_recv()
-        comb[j] = (acc[j, core] + half_got[j].astype(jnp.float32)).astype(jnp.bfloat16)
+        comb[j] = (acc[core, j] + half_got[j].astype(jnp.float32)).astype(jnp.bfloat16)
         final_copy(j, back(j)).start()
 
     def sent_early():
@@ -525,12 +545,23 @@
 
         tau = t - d_start
 
-        @pl.when(tau >= 0)
-        def _():
-            multiply_down(tau)
+        j, first = piece_of(jnp.maximum(tau, 0))
+        soon = tau < chips * early
+
+        @pl.when((tau >= 0) & soon & (j == 0))
+        def _():
+            multiply_down(first, 0, chips)
+
+        @pl.when(jnp.logical_not(soon) & (j == chips - 2))
+        def _():
+            multiply_down(first, chips - 2, 2)
+
+        @pl.when(jnp.logical_not(soon) & (j < chips - 2))
+        def _():
+            multiply_down(first, j, 1)
 
         for j in range(chips - 1, 0, -1):
-            done = chips * early + (chips - j) * late
+            done = chips * early + (chips - min(j, chips - 2)) * late
 
             @pl.when(tau == done - 1)
             def _():
@@ -548,9 +579,9 @@
 
     lax.fori_loop(0, d_start + steps, tick, 0)
 
-    half_send[0] = acc[0, 1 - core].astype(jnp.bfloat16)
+    half_send[0] = acc[1 - core, 0].astype(jnp.bfloat16)
     half_copy(0).start()
-    total = acc[0, core]
+    total = acc[core, 0]
     for j in range(1, chips):
         final_copy(back(j), j).wait_recv()
         total = total + final_got[j].astype(jnp.float32)
@@ -616,14 +647,14 @@
             pltpu.VMEM((chunks, tokens_all, 2 * GROUP), bf16),
             pltpu.VMEM((2, chunks, half, 2 * GROUP), bf16),
             pltpu.VMEM((2, chips, chunks, count, GROUP), bf16),
-            pltpu.VMEM((chips, 2, count, model), f32),
+            pltpu.VMEM((2, chips, count, model), f32),
             pltpu.VMEM((chips, count, model), bf16),
             pltpu.VMEM((chips, count, model), bf16),
             pltpu.VMEM((chips, count, model), bf16),
             pltpu.VMEM((chips, count, model), bf16),
             DMA((5 + 2 * parts,)),
-            DMA((2 * chips,)),
-            DMA((2 * chips,)),
+            DMA((4 * chips,)),
+            DMA((4 * chips,)),
             DMA((chips,)),
             DMA((chips,)),
             DMA((3,)),

time: 95.2 us -> 94.3 us (level)
  Pallas kernels: 91.5 us -> 90.5 us
where the time goes in v4:
time: 94.3 us; the launch traced here: 94.1 us
  Pallas kernels  90.5 us (96%)
  local copies, waits for them, and re-layouts  3.58 us (4%)
    pallas_call x1, Pallas kernels, layer(): pl.pallas_call(functools.partial(layer_kernel, rows, cols, chunks), in_sp...  90.5 us
    unnamed x2, local copies, waits for them, and re-layouts  3.58 us

profile of v4, /device:TPU:0, one launch (start us, length us, event | category | flops | bytes accessed | tf_op | source)
XLA Modules:
  0.0 94.1 jit_solution(8223148544247401963)
XLA Ops:
  0.0 2.0 %copy.8.down_scale = bf16[1024,224]{1,0:T(8,128)(2,1)} copy(bf16[1024,224]{0,1:T(8,128)(2,1)} %param.13) | data formatting | bytes 917504 | tf_op args[6]
  2.0 90.5 %layer.1 = bf16[32,2048]{1,0:T(8,128)(2,1)} custom-call(bf16[32,2048]{1,0:T(8,128)(2,1)} %tokens.1, s32[256,3584]{1,0:T(8,128)} %gate.1, s32[256,3584]{1,0:T(8,128)} %up.1, s32[448,2048]{1,0:T(8,128)} %down.1, bf16[8,28672]{1,0:T(8,128)(2,1)} %gate_scale.1, bf16[8,28672]{1,0:T(8,128)(2,1)} %up_scale.1, bf16[1024,224]{1,0:T(8,128)(2,1)} %copy.8.down_scale), custom_call_target="tpu_custom_call" | custom-call | tf_op jit(solution)/shard_map/layer/pallas_call | solution.py:625
  92.5 1.6 %copy.10 = bf16[32,2048]{1,0:T(8,128)(2,1)} copy(bf16[32,2048]{1,0:T(8,128)(2,1)} %layer.1) | data formatting | bytes 262144
